TPU v7x, 32 devices: a whole 2x2x4 slice. The times are simulated.
32 devices in a mesh: fsdp: 8 (over z, y), tp: 4 (over x, core).
Axes of the slice: x: 2, y: 2, z: 4, core: 2. Of those that a mesh axis runs over, the one named last changes fastest.
Arguments:
- inputs: bfloat16 [2, 4096, 1280], P(None, ('fsdp', 'tp')), may hold values from -6 to 6
- cotangent: bfloat16 [2, 4096, 1280], P(None, ('fsdp', 'tp')), may hold values from -6 to 6
- segment_ids: int32 [2, 4096], P(None, 'fsdp'), may hold values from 0 to 103, as said below
- parents: int32 [2, 104], P(None, 'fsdp'), may hold values from 0 to 103, as said below
- positions: int32 [2, 4096], P(None, 'fsdp'), may hold values from 0 to 191, as said below
- norm1_gain: bfloat16 [1280], P(('fsdp', 'tp')), may hold values from 0.5 to 1.5
- w_query: bfloat16 [1280, 1280], P('fsdp', 'tp'), may hold values from -0.15625 to 0.15625
- w_key: bfloat16 [1280, 320], P(('fsdp', 'tp')), may hold values from -0.15625 to 0.15625
- w_value: bfloat16 [1280, 320], P(('fsdp', 'tp')), may hold values from -0.15625 to 0.15625
- w_out: bfloat16 [1280, 1280], P('tp', 'fsdp'), may hold values from -0.625 to 0.625
- norm2_gain: bfloat16 [1280], P(('fsdp', 'tp')), may hold values from 0.5 to 1.5
- w_gate: bfloat16 [1280, 3584], P('fsdp', 'tp'), may hold values from -0.15625 to 0.15625
- w_up: bfloat16 [1280, 3584], P('fsdp', 'tp'), may hold values from -0.15625 to 0.15625
- w_down: bfloat16 [3584, 1280], P('tp', 'fsdp'), may hold values from -0.09375 to 0.09375
Outputs:
- output: bfloat16 [2, 4096, 1280], P(None, ('fsdp', 'tp'))
- grad_input: float32 [2, 4096, 1280], P(None, ('fsdp', 'tp'))
- grad_norm1: float32 [1280], P(('fsdp', 'tp'))
- grad_query: float32 [1280, 1280], P('fsdp', 'tp')
- grad_key: float32 [1280, 320], P(('fsdp', 'tp'))
- grad_value: float32 [1280, 320], P(('fsdp', 'tp'))
- grad_out: float32 [1280, 1280], P('tp', 'fsdp')
- grad_norm2: float32 [1280], P(('fsdp', 'tp'))
- grad_gate: float32 [1280, 3584], P('fsdp', 'tp')
- grad_up: float32 [1280, 3584], P('fsdp', 'tp')
- grad_down: float32 [3584, 1280], P('tp', 'fsdp')
Inputs may be any that keep to these rules, and one draw needn't show every extreme that they name: `segment_ids`: each tree of 512 consecutive tokens holds 13 segments: a trunk of 128 tokens, 4 branches and 8 leaves of 32 tokens each, two leaves on each branch. The segments of tree t are numbered 13 t to 13 t + 12 in an order drawn anew for every tree, the trunk first in the layout and the others in a drawn order. The parent of a trunk is the trunk itself, of a branch its tree's trunk, of a leaf its branch; parents stay in their segment's tree. `positions`: positions count along a token's path: a trunk from 0, a branch from 128, a leaf from 160, rising by one within a segment in token order.
All inputs are finite; a program needn't handle non-finite values.
Results may differ from a plain program's by a relative error of at most 0.018.
Values may be sent and summed in bfloat16 or wider, within the bound.
A program may use at most 128 MiB of HBM per device.

v0:
```python
import jax
import jax.numpy as jnp
from jax import lax
from jax.sharding import PartitionSpec as P

H = 20
KV = 5
HD = 64
MB = 2


EPSILON = 1e-05
ROPE_BASE = 10000.0
MASKED = -1e30


def across_rows(left_side, right_side):
    return lax.dot_general(
        left_side, right_side, (((0,), (0,)), ((), ())), preferred_element_type=jnp.float32
    )


def against_rows(left_side, right_side):
    return lax.dot_general(
        left_side, right_side, (((1,), (1,)), ((), ())), preferred_element_type=jnp.float32
    )


def norm_scale(values):
    return lax.rsqrt(jnp.mean(values * values, axis=-1, keepdims=True) + EPSILON)


def rotate(values, places, turning):
    half_width = HD // 2
    frequency = 1.0 / ROPE_BASE ** (jnp.arange(half_width, dtype=jnp.float32) / half_width)
    angles = places.astype(jnp.float32)[..., None] * frequency
    cosine = jnp.cos(angles)[..., None, :]
    sine_part = turning * jnp.sin(angles)[..., None, :]
    shaped = values.reshape(values.shape[:-1] + (values.shape[-1] // HD, HD))
    first_half = shaped[..., :half_width]
    second_half = shaped[..., half_width:]
    turned = jnp.concatenate(
        [
            first_half * cosine - second_half * sine_part,
            second_half * cosine + first_half * sine_part,
        ],
        axis=-1,
    )
    return turned.reshape(values.shape)


def lineage(segment, table):
    labels = jnp.arange(13, dtype=jnp.int32)
    first_label = jnp.min(segment) // 13 * 13
    picked = (segment - first_label)[:, None] == labels[None, :]
    parent = jnp.sum(jnp.where(picked, table[None, :], 0), axis=1)
    picked_two = (parent - first_label)[:, None] == labels[None, :]
    grand_parent = jnp.sum(jnp.where(picked_two, table[None, :], 0), axis=1)
    return (parent, grand_parent)


def allowed_pairs(block_segment, block_parent, block_grand, block_places, segment, places):
    same_path = (
        (segment[None, :] == block_segment[:, None])
        | (segment[None, :] == block_parent[:, None])
        | (segment[None, :] == block_grand[:, None])
    )
    return same_path & (places[None, :] <= block_places[:, None])


def rows_in(values):
    return lax.all_gather(values, "tp", axis=0, tiled=True)


def rows_out(term):
    return lax.psum_scatter(
        term.astype(jnp.bfloat16), "tp", scatter_dimension=0, tiled=True
    ).astype(jnp.float32)


def fetch_weights(w_query, w_out, w_key, w_value, norm1_gain, norm2_gain, w_gate, w_up, w_down):
    query_full, out_full = (
        lax.all_gather(w_query, "fsdp", axis=0, tiled=True),
        lax.all_gather(w_out, "fsdp", axis=1, tiled=True),
    )
    key_full, value_full, gain_one, gain_two = (
        lax.all_gather(w_key, ("fsdp", "tp"), axis=0, tiled=True),
        lax.all_gather(w_value, ("fsdp", "tp"), axis=0, tiled=True),
        lax.all_gather(norm1_gain, ("fsdp", "tp"), axis=0, tiled=True),
        lax.all_gather(norm2_gain, ("fsdp", "tp"), axis=0, tiled=True),
    )
    gate_full, up_full, down_full = (
        lax.all_gather(w_gate, "fsdp", axis=0, tiled=True),
        lax.all_gather(w_up, "fsdp", axis=0, tiled=True),
        lax.all_gather(w_down, "fsdp", axis=1, tiled=True),
    )
    return (
        query_full,
        key_full,
        value_full,
        out_full,
        gain_one.astype(jnp.float32),
        gain_two.astype(jnp.float32),
        gate_full,
        up_full,
        down_full,
    )


def reduce_grads(gradients):
    grad_q, grad_k, grad_v, grad_o, grad_g1, grad_g2, grad_gt, grad_u, grad_dn = gradients
    part_q, part_o, part_gt, part_u, part_dn = (
        lax.psum_scatter(grad_q, "fsdp", scatter_dimension=0, tiled=True),
        lax.psum_scatter(grad_o, "fsdp", scatter_dimension=1, tiled=True),
        lax.psum_scatter(grad_gt, "fsdp", scatter_dimension=0, tiled=True),
        lax.psum_scatter(grad_u, "fsdp", scatter_dimension=0, tiled=True),
        lax.psum_scatter(grad_dn, "fsdp", scatter_dimension=1, tiled=True),
    )
    part_k, part_v, part_g1, part_g2 = (
        lax.psum_scatter(grad_k, ("fsdp", "tp"), scatter_dimension=0, tiled=True),
        lax.psum_scatter(grad_v, ("fsdp", "tp"), scatter_dimension=0, tiled=True),
        lax.psum_scatter(grad_g1, ("fsdp", "tp"), scatter_dimension=0, tiled=True),
        lax.psum_scatter(grad_g2, ("fsdp", "tp"), scatter_dimension=0, tiled=True),
    )
    return (part_q, part_k, part_v, part_o, part_g1, part_g2, part_gt, part_u, part_dn)


def attention_forward(query_heads, keys_heads, values_heads, segment, parent, grand_parent, places):
    group_rows, local_heads = (query_heads.shape[0], query_heads.shape[1])
    block_rows = min(512, group_rows)
    block_count = group_rows // block_rows
    scale = HD ** (-0.5)

    def one_block(pieces):
        query_block, block_segment, block_parent, block_grand, block_places = pieces
        allowed = allowed_pairs(
            block_segment, block_parent, block_grand, block_places, segment, places
        )
        scores = (
            jnp.einsum("qhd,khd->hqk", query_block, keys_heads, preferred_element_type=jnp.float32)
            * scale
        )
        scores = jnp.where(allowed[None], scores, MASKED)
        row_peak = jnp.max(scores, axis=-1, keepdims=True)
        weights_row = jnp.exp(scores - row_peak)
        row_total = jnp.sum(weights_row, axis=-1, keepdims=True)
        probability = weights_row / row_total
        mixed = jnp.einsum(
            "hqk,khd->qhd",
            probability.astype(jnp.bfloat16),
            values_heads,
            preferred_element_type=jnp.float32,
        )
        return (mixed.astype(jnp.bfloat16), (row_peak + jnp.log(row_total))[..., 0])

    pieces = (
        query_heads.reshape(block_count, block_rows, local_heads, HD),
        segment.reshape(block_count, block_rows),
        parent.reshape(block_count, block_rows),
        grand_parent.reshape(block_count, block_rows),
        places.reshape(block_count, block_rows),
    )
    mixed, log_total = lax.map(one_block, pieces)
    return (mixed.reshape(group_rows, local_heads * HD), log_total)


def attention_backward(
    query_heads,
    keys_heads,
    values_heads,
    grad_mixed,
    log_total,
    segment,
    parent,
    grand_parent,
    places,
):
    group_rows, local_heads = (query_heads.shape[0], query_heads.shape[1])
    block_rows = min(512, group_rows)
    block_count = group_rows // block_rows
    scale = HD ** (-0.5)

    def one_block(running, pieces):
        key_grad, value_grad = running
        (
            query_block,
            out_block,
            block_log,
            block_segment,
            block_parent,
            block_grand,
            block_places,
        ) = pieces
        allowed = allowed_pairs(
            block_segment, block_parent, block_grand, block_places, segment, places
        )
        scores = (
            jnp.einsum("qhd,khd->hqk", query_block, keys_heads, preferred_element_type=jnp.float32)
            * scale
        )
        probability = jnp.where(allowed[None], jnp.exp(scores - block_log[..., None]), 0.0)
        grad_prob = jnp.einsum(
            "qhd,khd->hqk", out_block, values_heads, preferred_element_type=jnp.float32
        )
        row_delta = jnp.sum(probability * grad_prob, axis=-1, keepdims=True)
        grad_score = (scale * probability * (grad_prob - row_delta)).astype(jnp.bfloat16)
        query_grad = jnp.einsum(
            "hqk,khd->qhd", grad_score, keys_heads, preferred_element_type=jnp.float32
        )
        key_grad = key_grad + jnp.einsum(
            "hqk,qhd->khd", grad_score, query_block, preferred_element_type=jnp.float32
        )
        value_grad = value_grad + jnp.einsum(
            "hqk,qhd->khd",
            probability.astype(jnp.bfloat16),
            out_block,
            preferred_element_type=jnp.float32,
        )
        return ((key_grad, value_grad), query_grad)

    zeros_heads = jnp.zeros((group_rows, local_heads, HD), jnp.float32)
    pieces = (
        query_heads.reshape(block_count, block_rows, local_heads, HD),
        grad_mixed.reshape(block_count, block_rows, local_heads, HD),
        log_total,
        segment.reshape(block_count, block_rows),
        parent.reshape(block_count, block_rows),
        grand_parent.reshape(block_count, block_rows),
        places.reshape(block_count, block_rows),
    )
    (key_grad, value_grad), query_grad = lax.scan(one_block, (zeros_heads, zeros_heads), pieces)
    return (query_grad.reshape(group_rows, local_heads, HD), key_grad, value_grad)


def per_device(
    inputs,
    cotangent,
    segment_ids,
    parents,
    positions,
    norm1_gain,
    w_query,
    w_key,
    w_value,
    w_out,
    norm2_gain,
    w_gate,
    w_up,
    w_down,
):
    head_rank = lax.axis_index("tp")
    local_heads = w_query.shape[1] // HD
    key_head = (head_rank * local_heads + jnp.arange(local_heads, dtype=jnp.int32)) // (H // KV)
    head_choice = (key_head[:, None] == jnp.arange(KV, dtype=jnp.int32)[None, :]).astype(
        jnp.float32
    )
    choice_low = head_choice.astype(jnp.bfloat16)
    outputs = []
    input_grads = []
    shards = None
    for batch_index in range(MB):
        weights = fetch_weights(
            w_query, w_out, w_key, w_value, norm1_gain, norm2_gain, w_gate, w_up, w_down
        )
        (
            query_full,
            key_full,
            value_full,
            out_full,
            gain_one,
            gain_two,
            gate_full,
            up_full,
            down_full,
        ) = weights
        source = inputs[batch_index].astype(jnp.float32)
        segment = segment_ids[batch_index]
        places = positions[batch_index]
        parent, grand_parent = lineage(segment, parents[batch_index])
        norm_one = norm_scale(source)
        normed = (source * norm_one * gain_one).astype(jnp.bfloat16)
        normed_all = rows_in(normed)
        queries = rotate(
            jnp.dot(normed_all, query_full, preferred_element_type=jnp.float32), places, 1.0
        ).astype(jnp.bfloat16)
        keys_all = rotate(
            jnp.dot(normed_all, key_full, preferred_element_type=jnp.float32), places, 1.0
        ).astype(jnp.bfloat16)
        values_all = jnp.dot(normed_all, value_full, preferred_element_type=jnp.float32).astype(
            jnp.bfloat16
        )
        group_rows = keys_all.shape[0]
        keys_heads = jnp.einsum(
            "gkd,hk->ghd",
            keys_all.reshape(group_rows, KV, HD),
            choice_low,
            preferred_element_type=jnp.float32,
        ).astype(jnp.bfloat16)
        values_heads = jnp.einsum(
            "gkd,hk->ghd",
            values_all.reshape(group_rows, KV, HD),
            choice_low,
            preferred_element_type=jnp.float32,
        ).astype(jnp.bfloat16)
        query_heads = queries.reshape(group_rows, local_heads, HD)
        attended, log_total = attention_forward(
            query_heads, keys_heads, values_heads, segment, parent, grand_parent, places
        )
        hidden = source + rows_out(jnp.dot(attended, out_full, preferred_element_type=jnp.float32))
        norm_two = norm_scale(hidden)
        normed_two = (hidden * norm_two * gain_two).astype(jnp.bfloat16)
        normed_two_all = rows_in(normed_two)
        gate_pre = jnp.dot(normed_two_all, gate_full, preferred_element_type=jnp.float32)
        upward = jnp.dot(normed_two_all, up_full, preferred_element_type=jnp.float32)
        sigmoid_gate = jax.nn.sigmoid(gate_pre)
        activated = gate_pre * sigmoid_gate
        product = (activated * upward).astype(jnp.bfloat16)
        output = hidden + rows_out(jnp.dot(product, down_full, preferred_element_type=jnp.float32))
        grad_hidden = cotangent[batch_index].astype(jnp.float32)
        grad_branch = rows_in(grad_hidden.astype(jnp.bfloat16))
        grad_product = against_rows(grad_branch, down_full)
        grad_down_w = across_rows(product, grad_branch)
        grad_gate_pre = (
            grad_product * upward * sigmoid_gate * (1.0 + gate_pre * (1.0 - sigmoid_gate))
        ).astype(jnp.bfloat16)
        grad_upward = (grad_product * activated).astype(jnp.bfloat16)
        grad_gate_w = across_rows(normed_two_all, grad_gate_pre)
        grad_up_w = across_rows(normed_two_all, grad_upward)
        grad_normed_two = rows_out(
            against_rows(grad_gate_pre, gate_full) + against_rows(grad_upward, up_full)
        )
        gain_two_grad = jnp.sum(hidden * norm_two * grad_normed_two, axis=0)
        weighted_two = gain_two * grad_normed_two
        grad_hidden = (
            grad_hidden
            + norm_two * weighted_two
            - hidden
            * (norm_two * norm_two * norm_two)
            * jnp.mean(hidden * weighted_two, axis=-1, keepdims=True)
        )
        grad_attn = rows_in(grad_hidden.astype(jnp.bfloat16))
        grad_out_w = across_rows(attended, grad_attn)
        grad_mixed = (
            against_rows(grad_attn, out_full)
            .astype(jnp.bfloat16)
            .reshape(group_rows, local_heads, HD)
        )
        query_grad, key_grad, value_grad = attention_backward(
            query_heads,
            keys_heads,
            values_heads,
            grad_mixed,
            log_total,
            segment,
            parent,
            grand_parent,
            places,
        )
        key_part = jnp.einsum(
            "ghd,hk->gkd", key_grad, head_choice, precision=lax.Precision.HIGHEST
        ).reshape(group_rows, KV * HD)
        value_part = jnp.einsum(
            "ghd,hk->gkd", value_grad, head_choice, precision=lax.Precision.HIGHEST
        ).reshape(group_rows, KV * HD)
        key_part = rotate(key_part, places, -1.0)
        query_raw = rotate(query_grad.reshape(group_rows, local_heads * HD), places, -1.0).astype(
            jnp.bfloat16
        )
        grad_query_w = across_rows(normed_all, query_raw)
        normed_term = against_rows(query_raw, query_full)
        grad_normed = lax.psum_scatter(
            normed_term.astype(jnp.bfloat16), "tp", scatter_dimension=0, tiled=True
        ).astype(jnp.float32)
        key_sum = lax.psum_scatter(
            key_part.astype(jnp.bfloat16), "tp", scatter_dimension=0, tiled=True
        )
        value_sum = lax.psum_scatter(
            value_part.astype(jnp.bfloat16), "tp", scatter_dimension=0, tiled=True
        )
        grad_key_w = across_rows(normed, key_sum)
        grad_value_w = across_rows(normed, value_sum)
        grad_normed = (
            grad_normed + against_rows(key_sum, key_full) + against_rows(value_sum, value_full)
        )
        gain_one_grad = jnp.sum(source * norm_one * grad_normed, axis=0)
        weighted_one = gain_one * grad_normed
        grad_source = (
            grad_hidden
            + norm_one * weighted_one
            - source
            * (norm_one * norm_one * norm_one)
            * jnp.mean(source * weighted_one, axis=-1, keepdims=True)
        )
        gradients = (
            grad_query_w,
            grad_key_w,
            grad_value_w,
            grad_out_w,
            gain_one_grad,
            gain_two_grad,
            grad_gate_w,
            grad_up_w,
            grad_down_w,
        )
        output, grad_source, gradients = (output.astype(jnp.bfloat16), grad_source, gradients)
        outputs.append(output)
        input_grads.append(grad_source)
        summed = reduce_grads(gradients)
        shards = summed if batch_index == 0 else jax.tree.map(jnp.add, shards, summed)
    return (
        jnp.stack(outputs),
        jnp.stack(input_grads),
        shards[4],
        shards[0],
        shards[1],
        shards[2],
        shards[3],
        shards[5],
        shards[6],
        shards[7],
        shards[8],
    )


def solution(mesh):
    placed = (
        P(None, ("fsdp", "tp"), None),
        P(None, ("fsdp", "tp"), None),
        P(None, "fsdp"),
        P(None, "fsdp"),
        P(None, "fsdp"),
        P(("fsdp", "tp")),
        P("fsdp", "tp"),
        P(("fsdp", "tp"), None),
        P(("fsdp", "tp"), None),
        P("tp", "fsdp"),
        P(("fsdp", "tp")),
        P("fsdp", "tp"),
        P("fsdp", "tp"),
        P("tp", "fsdp"),
    )
    return jax.shard_map(
        per_device,
        mesh=mesh,
        in_specs=placed,
        out_specs=(
            P(None, ("fsdp", "tp"), None),
            P(None, ("fsdp", "tp"), None),
            P(("fsdp", "tp")),
            P("fsdp", "tp"),
            P(("fsdp", "tp"), None),
            P(("fsdp", "tp"), None),
            P("tp", "fsdp"),
            P(("fsdp", "tp")),
            P("fsdp", "tp"),
            P("fsdp", "tp"),
            P("tp", "fsdp"),
        ),
        check_vma=False,
    )
```

profile of v0, /device:TPU:0, one launch (start us, length us, event | category | flops | bytes accessed | tf_op | source)
XLA Modules:
  0.0 1434.9 jit_solution(6118796550019123196)
XLA Ops:
  11.2 42.1 %all-reduce.7 = (bf16[1280]{0:T(1024)(128)(2,1)S(1)}, bf16[1280]{0:T(1024)(128)(2,1)S(1)}) all-reduce(bf16[1280]{0:T(1024)(128)(2,1)S(1)} %dynamic-update-slice, bf16[1280]{0:T(1024)(128)(2,1)S(1)} %dynamic-update-slice.1), channel_id=1, replica_groups=mesh['fsdp'=8,'tp'=4] {'fsdp','tp'}, use_global_device_ids=true, to_apply=%add | all-reduce | flops 2560 | bytes 10240
  61.8 32.7 %all_gather.63 = bf16[1280,320]{1,0:T(8,128)(2,1)S(1)} all-gather(bf16[160,320]{1,0:T(8,128)(2,1)S(1)} %copy-done.80), channel_id=1, replica_groups=mesh['fsdp'=8,'tp'=4] {'fsdp'}, dimensions={0}, use_global_device_ids=true | all-gather | bytes 921600 | tf_op jit(solution)/shard_map/all_gather | solution.py:83
  96.5 34.0 %all_gather.65 = bf16[320,1280]{0,1:T(8,128)(2,1)} all-gather(bf16[320,160]{0,1:T(8,128)(2,1)S(1)} %copy-done.81), channel_id=1, replica_groups=mesh['fsdp'=8,'tp'=4] {'fsdp'}, dimensions={1}, use_global_device_ids=true | all-gather | bytes 921600 | tf_op jit(solution)/shard_map/all_gather | solution.py:84
  130.6 43.6 %all_gather.64 = bf16[1280,320]{1,0:T(8,128)(2,1)S(1)} all-gather(bf16[40,320]{1,0:T(8,128)(2,1)S(1)} %copy-done.91), channel_id=1, replica_groups=mesh['fsdp'=8,'tp'=4] {'fsdp','tp'}, dimensions={0}, use_global_device_ids=true | all-gather | bytes 844800 | tf_op jit(solution)/shard_map/all_gather | solution.py:87
  174.2 42.5 %all_gather.62 = bf16[1280,320]{1,0:T(8,128)(2,1)} all-gather(bf16[40,320]{1,0:T(8,128)(2,1)S(1)} %copy-done.92), channel_id=1, replica_groups=mesh['fsdp'=8,'tp'=4] {'fsdp','tp'}, dimensions={0}, use_global_device_ids=true | all-gather | bytes 844800 | tf_op jit(solution)/shard_map/all_gather | solution.py:88
  246.3 10.8 reduce-scatter.32.cloned.1.call-done
  257.1 28.8 %reduce-scatter.36.cloned.1.call-done = bf16[128,1280]{1,0:T(8,128)(2,1)} async-done(((bf16[512,1280]{1,0:T(8,128)(2,1)}), bf16[128,1280]{1,0:T(8,128)(2,1)}) %reduce-scatter.36.cloned.1.call-update) | async-done | bytes 327696 | tf_op jit(solution)/shard_map/reduce_scatter | solution.py:76
  296.9 18.6 %all-gather.16.cloned.1.call-done = bf16[512,1280]{1,0:T(8,128)(2,1)} async-done(((bf16[128,1280]{1,0:T(8,128)(2,1)}), bf16[512,1280]{1,0:T(8,128)(2,1)}) %all-gather.16.cloned.1.call-update) | async-done | bytes 1310736 | tf_op jit(solution)/shard_map/all_gather | solution.py:72
  315.5 4.8 fusion.156
  320.3 48.4 %all-gather.18.cloned.1.call-done = bf16[1280,896]{1,0:T(8,128)(2,1)} async-done(((bf16[160,896]{1,0:T(8,128)(2,1)}), bf16[1280,896]{1,0:T(8,128)(2,1)}) %all-gather.18.cloned.1.call-update) | async-done | bytes 2293776 | tf_op jit(solution)/shard_map/all_gather | solution.py:93
  368.7 4.8 fusion.155
  373.5 13.4 all-gather.32.cloned.1.call-done
  386.9 53.4 %all-gather.22.cloned.1.call-done = bf16[896,1280]{0,1:T(8,128)(2,1)} async-done(((bf16[896,160]{0,1:T(8,128)(2,1)}), bf16[896,1280]{0,1:T(8,128)(2,1)}) %all-gather.22.cloned.1.call-update) | async-done | bytes 2293776 | tf_op jit(solution)/shard_map/all_gather | solution.py:95
  440.2 6.3 multiply_convert_fusion.4
  451.6 6.7 all-gather.26.cloned.1.call-done
  458.4 5.0 fusion.160
  466.1 17.9 %all-gather.34.cloned.1.call-done = bf16[1,512,1280]{2,1,0:T(8,128)(2,1)} async-done(((bf16[1,128,1280]{2,1,0:T(8,128)(2,1)}), bf16[1,512,1280]{2,1,0:T(8,128)(2,1)}) %all-gather.34.cloned.1.call-update) | async-done | bytes 1310736 | tf_op jit(solution)/shard_map/all_gather | solution.py:72
  484.0 6.3 multiply_convert_fusion.2
  495.3 4.6 convolution_convert_fusion.4
  500.0 4.7 convolution_convert_fusion.5
  505.2 16.6 %reduce-scatter.44.cloned.1.call-done = bf16[128,1280]{1,0:T(8,128)(2,1)} async-done(((bf16[512,1280]{1,0:T(8,128)(2,1)}), bf16[128,1280]{1,0:T(8,128)(2,1)}) %reduce-scatter.44.cloned.1.call-update) | async-done | bytes 327696 | tf_op jit(solution)/shard_map/reduce_scatter | solution.py:76
  525.1 25.7 %reduce-scatter.38.cloned.1.call-done = bf16[128,1280]{1,0:T(8,128)(2,1)} async-done(((bf16[512,1280]{1,0:T(8,128)(2,1)}), bf16[128,1280]{1,0:T(8,128)(2,1)}) %reduce-scatter.38.cloned.1.call-update) | async-done | bytes 327696 | tf_op jit(solution)/shard_map/reduce_scatter | solution.py:76
  550.7 29.0 %reduce-scatter.34.cloned.1.call-done = bf16[128,1280]{1,0:T(8,128)(2,1)} async-done(((bf16[512,1280]{1,0:T(8,128)(2,1)}), bf16[128,1280]{1,0:T(8,128)(2,1)}) %reduce-scatter.34.cloned.1.call-update) | async-done | bytes 327696 | tf_op jit(solution)/shard_map/reduce_scatter | solution.py:76
  579.7 3.6 fusion.143
  585.0 16.7 %all-gather.28.cloned.1.call-done = bf16[512,1280]{1,0:T(8,128)(2,1)} async-done(((bf16[128,1280]{1,0:T(8,128)(2,1)}), bf16[512,1280]{1,0:T(8,128)(2,1)}) %all-gather.28.cloned.1.call-update) | async-done | bytes 1310736 | tf_op jit(solution)/shard_map/all_gather | solution.py:72
  604.0 4.6 multiply_reduce_fusion.1
  614.9 6.4 all-gather.30.cloned.1.call-done
  623.5 3.8 fusion.26
  641.3 6.7 multiply_reduce_fusion
  648.1 7.4 multiply_convert_fusion
  674.4 5.5 reduce-scatter.64.cloned.1.call-done
  683.5 20.3 %reduce-scatter.58.cloned.1.call-done = bf16[128,320]{1,0:T(8,128)(2,1)} async-done(((bf16[512,320]{1,0:T(8,128)(2,1)}), bf16[128,320]{1,0:T(8,128)(2,1)}) %reduce-scatter.58.cloned.1.call-update) | async-done | bytes 81936
  706.5 21.1 %reduce-scatter.62.cloned.1.call-done = bf16[128,320]{1,0:T(8,128)(2,1)} async-done(((bf16[512,320]{1,0:T(8,128)(2,1)}), bf16[128,320]{1,0:T(8,128)(2,1)}) %reduce-scatter.62.cloned.1.call-update) | async-done | bytes 81936
  727.6 3.4 convolution_add_fusion.7
  738.0 3.5 convolution_add_fusion.8
  741.7 3.3 fusion.19
  745.0 3.7 convolution_add_fusion
  752.9 3.7 convolution_add_fusion.1
  760.9 3.8 convolution_add_fusion.2
  769.0 16.8 %reduce-scatter.46.cloned.1.call-done = bf16[128,1280]{1,0:T(8,128)(2,1)} async-done(((bf16[512,1280]{1,0:T(8,128)(2,1)}), bf16[128,1280]{1,0:T(8,128)(2,1)}) %reduce-scatter.46.cloned.1.call-update) | async-done | bytes 327696 | tf_op jit(solution)/shard_map/reduce_scatter | solution.py:371
  789.2 39.4 %all-reduce.6 = (f32[1280]{0:T(1024)S(1)}, f32[1280]{0:T(1024)S(1)}) all-reduce(f32[1280]{0:T(1024)S(1)} %add.305, f32[1280]{0:T(1024)S(1)} %add.310), channel_id=25, replica_groups=mesh['fsdp'=8,'tp'=4] {'fsdp','tp'}, use_global_device_ids=true, to_apply=%region_33.34.clone | all-reduce | flops 2560 | bytes 20480
  832.7 57.8 %reduce-scatter.68.cloned.1.call-done = f32[40,320]{1,0:T(8,128)} async-done(((f32[1280,320]{1,0:T(8,128)}), f32[40,320]{1,0:T(8,128)}) %reduce-scatter.68.cloned.1.call-update) | async-done | bytes 51216
  890.5 103.7 %reduce-scatter.66.cloned.1.call-done = f32[40,320]{1,0:T(8,128)} async-done(((f32[1280,320]{1,0:T(8,128)}), f32[40,320]{1,0:T(8,128)}) %reduce-scatter.66.cloned.1.call-update) | async-done | bytes 51216
  994.2 70.6 %reduce-scatter.50.cloned.1.call-done = f32[320,160]{0,1:T(8,128)} async-done(((f32[320,1280]{0,1:T(8,128)}), f32[320,160]{0,1:T(8,128)}) %reduce-scatter.50.cloned.1.call-update) | async-done | bytes 204816 | tf_op jit(solution)/shard_map/reduce_scatter | solution.py:114
  1064.8 70.2 %reduce-scatter.48.cloned.1.call-done = f32[160,320]{1,0:T(8,128)} async-done(((f32[1280,320]{1,0:T(8,128)}), f32[160,320]{1,0:T(8,128)}) %reduce-scatter.48.cloned.1.call-update) | async-done | bytes 204816 | tf_op jit(solution)/shard_map/reduce_scatter | solution.py:113
  1135.0 96.9 %reduce-scatter.56.cloned.1.call-done = f32[896,160]{0,1:T(8,128)} async-done(((f32[896,1280]{0,1:T(8,128)}), f32[896,160]{0,1:T(8,128)}) %reduce-scatter.56.cloned.1.call-update) | async-done | bytes 573456 | tf_op jit(solution)/shard_map/reduce_scatter | solution.py:117
  1231.9 97.6 %reduce-scatter.54.cloned.1.call-done = f32[160,896]{1,0:T(8,128)} async-done(((f32[1280,896]{1,0:T(8,128)}), f32[160,896]{1,0:T(8,128)}) %reduce-scatter.54.cloned.1.call-update) | async-done | bytes 573456 | tf_op jit(solution)/shard_map/reduce_scatter | solution.py:116
  1329.5 97.7 %reduce-scatter.52.cloned.1.call-done = f32[160,896]{1,0:T(8,128)} async-done(((f32[1280,896]{1,0:T(8,128)}), f32[160,896]{1,0:T(8,128)}) %reduce-scatter.52.cloned.1.call-update) | async-done | bytes 573456 | tf_op jit(solution)/shard_map/reduce_scatter | solution.py:115
  (406 shorter events, 144.4 us)
Async XLA Ops:
  8.0 48.8 %copy-start.97 = (s32[2,512]{1,0:T(2,128)S(1)}, s32[2,512]{1,0:T(2,128)}, u32[]{:S(2)}) copy-start(s32[2,512]{1,0:T(2,128)} %param.16) | copy-start | bytes 12292
  8.0 53.3 %copy-start.101 = (s32[2,13]{1,0:T(2,128)S(1)}, s32[2,13]{1,0:T(2,128)}, u32[]{:S(2)}) copy-start(s32[2,13]{1,0:T(2,128)} %param.17) | copy-start | bytes 316
  8.0 53.4 %copy-start.98 = (s32[2,512]{1,0:T(2,128)S(1)}, s32[2,512]{1,0:T(2,128)}, u32[]{:S(2)}) copy-start(s32[2,512]{1,0:T(2,128)} %param.18) | copy-start | bytes 12292
  8.0 53.8 %copy-start.80 = (bf16[160,320]{1,0:T(8,128)(2,1)S(1)}, bf16[160,320]{1,0:T(8,128)(2,1)}, u32[]{:S(2)}) copy-start(bf16[160,320]{1,0:T(8,128)(2,1)} %param.20) | copy-start | bytes 307204
  8.1 208.6 %all-gather.24.cloned.1.call-start = ((), (), s32[]{:S(2)}) async-start(), calls=%async_computation.26 | async-start | bytes 1638400 | tf_op jit(solution)/shard_map/all_gather | solution.py:72
  8.1 88.4 %copy-start.81 = (bf16[320,160]{0,1:T(8,128)(2,1)S(1)}, bf16[320,160]{0,1:T(8,128)(2,1)}, u32[]{:S(2)}) copy-start(bf16[320,160]{0,1:T(8,128)(2,1)} %param.23) | copy-start | bytes 307204
  53.2 43.3 %copy-start.78 = (f32[1280]{0:T(1024)}, f32[1280]{0:T(1024)S(1)}, u32[]{:S(2)}) copy-start(f32[1280]{0:T(1024)S(1)} %convert_element_type.264) | copy-start | bytes 15364
  53.8 42.7 %copy-start.93 = (f32[128]{0:T(128)}, f32[128]{0:T(128)S(1)}, u32[]{:S(2)}) copy-start(f32[128]{0:T(128)S(1)} %get-tuple-element.240) | copy-start | bytes 1540
  53.8 42.7 %copy-start.95 = (f32[128]{0:T(128)}, f32[128]{0:T(128)S(1)}, u32[]{:S(2)}) copy-start(f32[128]{0:T(128)S(1)} %get-tuple-element.257) | copy-start | bytes 1540
  56.0 74.6 %copy-start.91 = (bf16[40,320]{1,0:T(8,128)(2,1)S(1)}, bf16[40,320]{1,0:T(8,128)(2,1)}, u32[]{:S(2)}) copy-start(bf16[40,320]{1,0:T(8,128)(2,1)} %param.21) | copy-start | bytes 76804
  56.0 162.7 %all-gather.14.cloned.1.call-start = ((), (), s32[]{:S(2)}) async-start(), calls=%async_computation.19 | async-start | bytes 1638400 | tf_op jit(solution)/shard_map/all_gather | solution.py:72
  56.0 118.1 %copy-start.92 = (bf16[40,320]{1,0:T(8,128)(2,1)S(1)}, bf16[40,320]{1,0:T(8,128)(2,1)}, u32[]{:S(2)}) copy-start(bf16[40,320]{1,0:T(8,128)(2,1)} %param.22) | copy-start | bytes 76804
  56.7 200.4 %reduce-scatter.32.cloned.1.call-start = ((), (), s32[]{:S(2)}) async-start(), calls=%async_computation.20 | async-start | bytes 1638400 | tf_op jit(solution)/shard_map/reduce_scatter | solution.py:76
  94.9 133.4 %copy-start.22 = (pred[512,512]{0,1:T(8,128)(4,1)}, pred[512,512]{0,1:T(8,128)(4,1)S(1)}, u32[]{:S(2)}) copy-start(pred[512,512]{0,1:T(8,128)(4,1)S(1)} %compare_and_fusion.1) | copy-start | bytes 786436
  95.2 141.4 %copy-start.86 = (s32[5]{0:T(128)}, s32[5]{0:T(128)S(1)}, u32[]{:S(2)}) copy-start(s32[5]{0:T(128)S(1)} %and_select_fusion) | copy-start | bytes 64
  96.5 136.8 %copy-start.63 = (f32[512,32]{0,1:T(8,128)}, f32[512,32]{0,1:T(8,128)S(1)}, u32[]{:S(2)}) copy-start(f32[512,32]{0,1:T(8,128)S(1)} %get-tuple-element.242) | copy-start | bytes 196612
  233.1 52.9 %reduce-scatter.36.cloned.1.call-start = ((), (), s32[]{:S(2)}) async-start(), calls=%async_computation.27 | async-start | bytes 1638400 | tf_op jit(solution)/shard_map/reduce_scatter | solution.py:76
  242.9 43.1 %copy-start.2 = (bf16[2,128,1280]{2,1,0:T(8,128)(2,1)S(1)}, bf16[2,128,1280]{2,1,0:T(8,128)(2,1)}, u32[]{:S(2)}) copy-start(bf16[2,128,1280]{2,1,0:T(8,128)(2,1)} %param.14) | copy-start | bytes 1966084
  245.6 45.5 %copy-start.28 = (bf16[2,128,1280]{2,1,0:T(8,128)(2,1)S(1)}, bf16[2,128,1280]{2,1,0:T(8,128)(2,1)}, u32[]{:S(2)}) copy-start(bf16[2,128,1280]{2,1,0:T(8,128)(2,1)} %param.15) | copy-start | bytes 1966084
  245.7 51.2 %all-gather.20.cloned.1.call-start = ((), (), s32[]{:S(2)}) async-start(), calls=%async_computation.23 | async-start | bytes 2580480 | tf_op jit(solution)/shard_map/all_gather | solution.py:94
  246.2 69.3 %all-gather.16.cloned.1.call-start = ((), (), s32[]{:S(2)}) async-start(), calls=%async_computation.21 | async-start | bytes 1638400 | tf_op jit(solution)/shard_map/all_gather | solution.py:72
  290.6 78.1 %all-gather.18.cloned.1.call-start = ((), (), s32[]{:S(2)}) async-start(), calls=%async_computation.22 | async-start | bytes 2580480 | tf_op jit(solution)/shard_map/all_gather | solution.py:93
  291.1 95.7 %all-gather.32.cloned.1.call-start = ((), (), s32[]{:S(2)}) async-start(), calls=%async_computation.36 | async-start | bytes 1638400 | tf_op jit(solution)/shard_map/all_gather | solution.py:72
  292.1 148.1 %all-gather.22.cloned.1.call-start = ((), (), s32[]{:S(2)}) async-start(), calls=%async_computation.24 | async-start | bytes 2580480 | tf_op jit(solution)/shard_map/all_gather | solution.py:95
  292.9 165.5 %all-gather.26.cloned.1.call-start = ((), (), s32[]{:S(2)}) async-start(), calls=%async_computation.28 | async-start | bytes 1638400 | tf_op jit(solution)/shard_map/all_gather | solution.py:72
  293.6 190.4 %all-gather.34.cloned.1.call-start = ((), (), s32[]{:S(2)}) async-start(), calls=%async_computation.37 | async-start | bytes 1638400 | tf_op jit(solution)/shard_map/all_gather | solution.py:72
  294.2 211.0 %reduce-scatter.40.cloned.1.call-start = ((), (), s32[]{:S(2)}) async-start(), calls=%async_computation.30 | async-start | bytes 1638400 | tf_op jit(solution)/shard_map/reduce_scatter | solution.py:76
  451.6 70.2 %reduce-scatter.44.cloned.1.call-start = ((), (), s32[]{:S(2)}) async-start(), calls=%async_computation.33 | async-start | bytes 1638400 | tf_op jit(solution)/shard_map/reduce_scatter | solution.py:76
  495.3 55.5 %reduce-scatter.38.cloned.1.call-start = ((), (), s32[]{:S(2)}) async-start(), calls=%async_computation.29 | async-start | bytes 1638400 | tf_op jit(solution)/shard_map/reduce_scatter | solution.py:76
  499.9 79.8 %reduce-scatter.34.cloned.1.call-start = ((), (), s32[]{:S(2)}) async-start(), calls=%async_computation.25 | async-start | bytes 1638400 | tf_op jit(solution)/shard_map/reduce_scatter | solution.py:76
  504.7 97.0 %all-gather.28.cloned.1.call-start = ((), (), s32[]{:S(2)}) async-start(), calls=%async_computation.31 | async-start | bytes 1638400 | tf_op jit(solution)/shard_map/all_gather | solution.py:72
  583.3 37.9 %all-gather.30.cloned.1.call-start = ((), (), s32[]{:S(2)}) async-start(), calls=%async_computation.34 | async-start | bytes 1638400 | tf_op jit(solution)/shard_map/all_gather | solution.py:72
  584.9 86.9 %reduce-scatter.60.cloned.1.call-start = ((), (), s32[]{:S(2)}) async-start(), calls=%async_computation.44 | async-start | bytes 491520
  635.9 44.1 %reduce-scatter.64.cloned.1.call-start = ((), (), s32[]{:S(2)}) async-start(), calls=%async_computation.46 | async-start | bytes 491520
  648.0 55.8 %reduce-scatter.58.cloned.1.call-start = ((), (), s32[]{:S(2)}) async-start(), calls=%async_computation.43 | async-start | bytes 491520
  662.7 64.9 %reduce-scatter.62.cloned.1.call-start = ((), (), s32[]{:S(2)}) async-start(), calls=%async_computation.45 | async-start | bytes 491520
  666.3 100.4 %reduce-scatter.42.cloned.1.call-start = ((), (), s32[]{:S(2)}) async-start(), calls=%async_computation.32 | async-start | bytes 1638400 | tf_op jit(solution)/shard_map/reduce_scatter | solution.py:371
  668.7 117.2 %reduce-scatter.46.cloned.1.call-start = ((), (), s32[]{:S(2)}) async-start(), calls=%async_computation.35 | async-start | bytes 1638400 | tf_op jit(solution)/shard_map/reduce_scatter | solution.py:371
  671.7 218.8 %reduce-scatter.68.cloned.1.call-start = ((), (), s32[]{:S(2)}) async-start(), calls=%async_computation.48 | async-start | bytes 2027520
  683.3 311.0 %reduce-scatter.66.cloned.1.call-start = ((), (), s32[]{:S(2)}) async-start(), calls=%async_computation.47 | async-start | bytes 2027520
  731.0 333.8 %reduce-scatter.50.cloned.1.call-start = ((), (), s32[]{:S(2)}) async-start(), calls=%async_computation.39 | async-start | bytes 2211840 | tf_op jit(solution)/shard_map/reduce_scatter | solution.py:114
  735.7 399.3 %reduce-scatter.48.cloned.1.call-start = ((), (), s32[]{:S(2)}) async-start(), calls=%async_computation.38 | async-start | bytes 2211840 | tf_op jit(solution)/shard_map/reduce_scatter | solution.py:113
  741.6 490.3 %reduce-scatter.56.cloned.1.call-start = ((), (), s32[]{:S(2)}) async-start(), calls=%async_computation.42 | async-start | bytes 5160960 | tf_op jit(solution)/shard_map/reduce_scatter | solution.py:117
  748.8 580.7 %reduce-scatter.54.cloned.1.call-start = ((), (), s32[]{:S(2)}) async-start(), calls=%async_computation.41 | async-start | bytes 5160960 | tf_op jit(solution)/shard_map/reduce_scatter | solution.py:116
  756.7 670.5 %reduce-scatter.52.cloned.1.call-start = ((), (), s32[]{:S(2)}) async-start(), calls=%async_computation.40 | async-start | bytes 5160960 | tf_op jit(solution)/shard_map/reduce_scatter | solution.py:115
  787.8 42.0 %copy-start.27 = (f32[128,1280]{1,0:T(8,128)S(1)}, f32[128,1280]{1,0:T(8,128)}, u32[]{:S(2)}) copy-start(f32[128,1280]{1,0:T(8,128)} %get-tuple-element.159) | copy-start | bytes 1966084
  787.8 42.0 %copy-start.99 = (f32[128]{0:T(128)S(1)}, f32[128]{0:T(128)}, u32[]{:S(2)}) copy-start(f32[128]{0:T(128)} %get-tuple-element.239) | copy-start | bytes 1540
  787.8 42.0 %copy-start.100 = (f32[128]{0:T(128)S(1)}, f32[128]{0:T(128)}, u32[]{:S(2)}) copy-start(f32[128]{0:T(128)} %get-tuple-element.258) | copy-start | bytes 1540
  (91 other events, 466.6 us)
Sparse Core Ops, SparseCore 0:
  56.1 17.9 all-gather.23
  75.7 18.1 all-gather.13
  233.2 23.8 reduce-scatter.31
  259.5 26.4 reduce-scatter.35
  451.7 25.2 reduce-scatter.39
  495.4 26.3 reduce-scatter.43
  524.3 26.3 reduce-scatter.37
  553.3 26.3 reduce-scatter.33
  583.5 18.1 all-gather.27
  603.1 18.1 all-gather.29
Sparse Core Ops, SparseCore 1:
  248.3 48.5 all-gather.19
  298.9 16.5 all-gather.15
  317.6 51.1 all-gather.17
  370.3 16.5 all-gather.31
  389.1 51.1 all-gather.21
  441.8 16.5 all-gather.25
  459.8 24.1 all-gather.33
  635.9 20.7 reduce-scatter.59
  659.1 20.7 reduce-scatter.63
  683.0 20.7 reduce-scatter.57
  706.8 20.7 reduce-scatter.61
  730.1 26.3 reduce-scatter.41
  759.5 26.3 reduce-scatter.45
  791.7 98.8 reduce-scatter.67
  896.4 97.8 reduce-scatter.65
  998.3 66.4 reduce-scatter.49
  1068.9 66.1 reduce-scatter.47
  1139.2 92.6 reduce-scatter.55
  1236.0 93.4 reduce-scatter.53
  1333.7 93.4 reduce-scatter.51
where the time goes:
time: 1440 us; the launch traced here: 1430 us
  waiting for transfers between devices  957 us (66%)
  blocking collectives  234 us (16%)
  matrix products  152 us (11%)
  other arithmetic  41.1 us (3%)
  local copies, waits for them, and re-layouts  26.5 us (2%)
  between operations  21.6 us (2%)
    unnamed x36, waiting for transfers between devices  212 us
    reduce_scatter x6, waiting for transfers between devices, rows_out(): lax.psum_scatter(term.astype(jnp.bfloat16), 'tp', scatter_dimension=0, ti...  111 us
    reduce_scatter x1, waiting for transfers between devices, reduce_grads(): lax.psum_scatter(grad_gt, 'fsdp', scatter_dimension=0, tiled=True)  97.7 us
    reduce_scatter x1, waiting for transfers between devices, reduce_grads(): lax.psum_scatter(grad_u, 'fsdp', scatter_dimension=0, tiled=True)  97.6 us
    reduce_scatter x1, waiting for transfers between devices, reduce_grads(): lax.psum_scatter(grad_dn, 'fsdp', scatter_dimension=1, tiled=True)  96.9 us
    unnamed x2, blocking collectives  81.5 us
    all_gather x8, waiting for transfers between devices, rows_in(): return lax.all_gather(values, 'tp', axis=0, tiled=True)  79.7 us
    reduce_scatter x1, waiting for transfers between devices, reduce_grads(): lax.psum_scatter(grad_o, 'fsdp', scatter_dimension=1, tiled=True)  70.6 us
  transfers between devices with their start and end apart: 30, of which 25 were waited for; matrix products, arithmetic and copies ran while one was open for 12% of the time, Pallas kernels for 0%

commit v1 on v0

--- a/solution.py
+++ b/solution.py
@@ -1,17 +1,897 @@
+import functools
+
 import jax
 import jax.numpy as jnp
 from jax import lax
+from jax.experimental import pallas as pl
+from jax.experimental.pallas import tpu as pltpu
 from jax.sharding import PartitionSpec as P
 
+EPSILON = 1e-05
+ROPE_BASE = 10000.0
+MASKED = -1e30
 H = 20
 KV = 5
 HD = 64
 MB = 2
-
-
-EPSILON = 1e-05
-ROPE_BASE = 10000.0
-MASKED = -1e30
+MESH = pl.DeviceIdType.MESH
+BF = jnp.bfloat16
+F32 = jnp.float32
+QKV = 640
+AW = 1024
+
+
+def dot(left, right, left_dim, right_dim):
+    return lax.dot_general(
+        left, right, (((left_dim,), (right_dim,)), ((), ())), preferred_element_type=F32
+    )
+
+
+def loop(count, body):
+    def step(index, carry):
+        body(index)
+        return carry
+
+    lax.fori_loop(0, count, step, 0)
+
+
+def rows(index, size, extent):
+    return pl.ds(pl.multiple_of(index * size, size), extent)
+
+
+def swap_halves(values):
+    lane = lax.broadcasted_iota(jnp.int32, values.shape, 1)
+    return jnp.where(lane % 64 < 32, pltpu.roll(values, 96, 1), pltpu.roll(values, 32, 1))
+
+
+class Exchange:
+    def __init__(self, k, tag, whole, base, source=None):
+        own, near, far = k.t, k.x * 2 + 1 - k.c, (1 - k.x) * 2 + k.c
+        self.whole = whole
+
+        def block(rank):
+            return whole.at[pl.ds(pl.multiple_of(base + rank * 128, 128), 128)]
+
+        src = block(own) if source is None else source
+        self.to_sib = pltpu.make_async_remote_copy(
+            src, block(own), k.ex_s.at[tag, 0], k.ex_r.at[tag, 0], (k.f, k.sib), MESH)
+        self.to_far = pltpu.make_async_remote_copy(
+            src, block(own), k.ex_s.at[tag, 1], k.ex_r.at[tag, 1], (k.f, k.far), MESH)
+        self.relay = pltpu.make_async_remote_copy(
+            block(far), block(far), k.ex_s.at[tag, 2], k.ex_r.at[tag, 2], (k.f, k.sib), MESH)
+
+    def start(self):
+        self.to_far.start()
+        self.to_sib.start()
+
+    def forward(self):
+        self.to_far.wait_recv()
+        self.relay.start()
+
+    def finish(self):
+        self.to_sib.wait_recv()
+        self.relay.wait_recv()
+
+    def drain(self):
+        self.to_far.wait_send()
+        self.to_sib.wait_send()
+        self.relay.wait_send()
+
+
+class TreeSum:
+    def __init__(self, k, tag, keep, b):
+        self.k, self.b, self.keep = k, b, keep
+        self.inner = pltpu.make_async_remote_copy(
+            k.part.at[b, 1 - k.c], k.near.at[keep, b], k.ts_s.at[tag, 0], k.ts_r.at[tag, 0], (k.f, k.sib), MESH)
+        self.outer = pltpu.make_async_remote_copy(
+            k.half.at[keep, b], k.far_in.at[keep, b], k.ts_s.at[tag, 1], k.ts_r.at[tag, 1], (k.f, k.far), MESH)
+
+    def start(self):
+        self.inner.start()
+
+    def middle(self):
+        k, b, keep = self.k, self.b, self.keep
+        self.inner.wait_recv()
+        other = 1 - k.x
+
+        def body(i):
+            r = rows(i, 32, 32)
+            k.half[keep, b, r, :] = (
+                k.part[b, k.c, other, r, :].astype(F32) + k.near[keep, b, other, r, :].astype(F32)
+            ).astype(BF)
+
+        loop(4, body)
+        self.outer.start()
+
+    def wait(self):
+        self.outer.wait_recv()
+
+    def value(self, r):
+        k, b, keep = self.k, self.b, self.keep
+        return (
+            k.part[b, k.c, k.x, r, :].astype(F32)
+            + k.near[keep, b, k.x, r, :].astype(F32)
+            + k.far_in[keep, b, r, :].astype(F32)
+        )
+
+    def drain(self):
+        self.inner.wait_send()
+        self.outer.wait_send()
+
+
+class RingGather:
+    def __init__(self, k, tag, whole, lane, width):
+        self.k, self.tag, self.whole, self.lane, self.width = k, tag, whole, lane, width
+        self.step = 0
+
+    def copy(self, way, s):
+        k = self.k
+        spot = k.at_ring((k.p + (k.n - s if way == 0 else s)) % k.n)
+        half = k.shard // 2
+        where = pl.ds(pl.multiple_of(spot * k.shard + way * half, 16), half)
+        ref = self.whole.at[where, pl.ds(self.lane, self.width)]
+        return pltpu.make_async_remote_copy(
+            ref, ref, k.ga_s.at[self.tag * 2 + way, s], k.ga_r.at[self.tag * 2 + way, s],
+            (k.next if way == 0 else k.prev, k.t), MESH)
+
+    def start(self):
+        for way in (0, 1):
+            self.copy(way, 0).start()
+
+    def pump(self):
+        s = self.step
+        self.step += 1
+        for way in (0, 1):
+            self.copy(way, s).wait_recv()
+            if s < self.k.n - 2:
+                self.copy(way, s + 1).start()
+
+    def drain(self):
+        if self.step:
+            self.step = 0
+            for s in range(self.k.n - 1):
+                for way in (0, 1):
+                    self.copy(way, s).wait_send()
+
+
+class RingSum:
+    def __init__(self, k, tag, grad, lane, width, slots, result, out_lane):
+        self.k, self.tag, self.grad, self.lane, self.width = k, tag, grad, lane, width
+        self.slots, self.result, self.out_lane = slots, result, out_lane
+        self.step = 0
+
+    def own(self, way, s):
+        k = self.k
+        spot = k.at_ring((k.p + (2 * k.n - 1 - s if way == 0 else 1 + s)) % k.n)
+        half = k.shard // 2
+        return pl.ds(pl.multiple_of(spot * k.shard + way * half, 16), half)
+
+    def copy(self, way, s):
+        k = self.k
+        if s == 0:
+            src = self.grad.at[self.own(way, 0), pl.ds(self.lane, self.width)]
+        else:
+            src = self.slots.at[way, s - 1, :, pl.ds(self.lane, self.width)]
+        return pltpu.make_async_remote_copy(
+            src, self.slots.at[way, s, :, pl.ds(self.lane, self.width)],
+            k.rs_s.at[self.tag * 2 + way, s], k.rs_r.at[self.tag * 2 + way, s],
+            (k.next if way == 0 else k.prev, k.t), MESH)
+
+    def start(self):
+        for way in (0, 1):
+            self.copy(way, 0).start()
+
+    def pump(self):
+        k, s = self.k, self.step
+        self.step += 1
+        lanes = pl.ds(self.lane, self.width)
+        for way in (0, 1):
+            self.copy(way, s).wait_recv()
+            total = self.slots[way, s, :, lanes].astype(F32) + self.grad[self.own(way, s + 1), lanes].astype(F32)
+            if s < k.n - 2:
+                self.slots[way, s, :, lanes] = total.astype(BF)
+                self.copy(way, s + 1).start()
+            else:
+                half = k.shard // 2
+                self.result[way * half:(way + 1) * half, self.out_lane:self.out_lane + self.width] = total
+
+    def drain(self):
+        for s in range(self.k.n - 1):
+            for way in (0, 1):
+                self.copy(way, s).wait_send()
+
+
+class Kernel:
+    pass
+
+
+def layer_kernel(n, shard, names, debug, stop, *refs):
+    k = Kernel()
+    for name, ref in zip(names, refs):
+        setattr(k, name, ref)
+    k.n, k.shard = n, shard
+    f, t = lax.axis_index("fsdp"), lax.axis_index("tp")
+    k.f, k.t, k.x, k.c = f, t, t // 2, t % 2
+    k.sib = k.x * 2 + 1 - k.c
+    k.far = (1 - k.x) * 2 + k.c
+    cross = (1 - k.x) * 2 + 1 - k.c
+    even = 1 - f % 2
+    k.p = even * (f // 2) + (1 - even) * (n - 1 - f // 2)
+
+    def at_ring(place):
+        high = place // (n // 2)
+        return (1 - high) * (2 * place) + high * (2 * (n - 1 - place) + 1)
+
+    k.at_ring = at_ring
+    k.next, k.prev = at_ring((k.p + 1) % n), at_ring((k.p + n - 1) % n)
+
+    barrier = pltpu.get_barrier_semaphore()
+    for peer in ((f, k.sib), (f, k.far), (f, cross), (k.next, t), (k.prev, t)):
+        pl.semaphore_signal(barrier, inc=1, device_id=peer, device_id_type=MESH)
+
+    mine = pl.ds(pl.multiple_of(f * shard, 16), shard)
+    locals_ = [
+        pltpu.make_async_copy(k.gate, k.wgu.at[mine, pl.ds(0, 896)], k.loc.at[0]),
+        pltpu.make_async_copy(k.up, k.wgu.at[mine, pl.ds(896, 896)], k.loc.at[1]),
+        pltpu.make_async_copy(k.down, k.wd.at[mine], k.loc.at[2]),
+    ]
+    token_copies = []
+    for b in range(MB):
+        own = pl.ds(pl.multiple_of(b * 512 + t * 128, 128), 128)
+        token_copies.append(pltpu.make_async_copy(k.xin.at[b], k.xall.at[own], k.loc.at[3 + b]))
+        token_copies.append(pltpu.make_async_copy(k.dyin.at[b], k.dyall.at[own], k.loc.at[5 + b]))
+    for copy in locals_ + token_copies:
+        copy.start()
+    pl.semaphore_wait(barrier, 5)
+
+    kv_copies = []
+    for i, peer in enumerate((k.sib, k.far, cross)):
+        kv_copies.append(pltpu.make_async_remote_copy(
+            k.kv4.at[peer], k.kvr.at[t], k.kv_s.at[i], k.kv_r.at[i], (f, peer), MESH))
+    own_kv = pltpu.make_async_copy(k.kv4.at[t], k.kvr.at[t], k.loc.at[7])
+    own_kv.start()
+    for copy in kv_copies:
+        copy.start()
+    ex = {}
+    for b in range(MB):
+        ex["x", b] = Exchange(k, b, k.xall, b * 512, k.xin.at[b])
+        ex["dy", b] = Exchange(k, 2 + b, k.dyall, b * 512, k.dyin.at[b])
+        ex["n2", b] = Exchange(k, 4 + b, k.n2all, b * 512)
+        ex["dh", b] = Exchange(k, 6 + b, k.dyall, b * 512)
+    for b in range(MB):
+        ex["x", b].start()
+    for copy in kv_copies:
+        copy.wait_recv()
+    own_kv.wait()
+
+    part_rows = shard // 4
+    for rank in range(4):
+        there = pl.ds(pl.multiple_of(f * shard + rank * part_rows, 8), part_rows)
+        here = slice(rank * part_rows, (rank + 1) * part_rows)
+        k.stage[here, 0:256] = k.kvr[rank, :, 0:256]
+        k.stage[here, 256:512] = k.apre[here, 256:512]
+        k.stage[here, 512:640] = k.apre[here, 512:640] + k.kvr[rank, :, 256:384]
+        k.stage[here, 640:1024] = k.apre[here, 640:1024]
+    to_wa = pltpu.make_async_copy(k.stage, k.wa.at[mine], k.loc.at[8])
+    to_wa.start()
+    to_wa.wait()
+    ring = {
+        "kvq": RingGather(k, 0, k.wa, 0, 640),
+        "o": RingGather(k, 1, k.wa, 640, 384),
+        "g": RingGather(k, 2, k.wgu, 0, 896),
+        "u": RingGather(k, 3, k.wgu, 896, 896),
+        "d": RingGather(k, 4, k.wd, 0, 896),
+    }
+    ring["kvq"].start()
+    ring["o"].start()
+    for copy in locals_:
+        copy.wait()
+
+    lane = lax.broadcasted_iota(jnp.int32, (8, 128), 1)[0:1]
+    for b in range(MB):
+        stacked = jnp.concatenate(
+            [k.seg[b:b + 1].astype(F32), k.pos[b:b + 1].astype(F32), jnp.zeros((126, 512), F32)], axis=0)
+        columns = stacked.T
+        seg_col, pos_col = columns[:, 0:1], columns[:, 1:2]
+        first = (f * 13).astype(F32)
+        parent = jnp.zeros((512, 1), F32)
+        for label in range(13):
+            parent = jnp.where(seg_col == first + label, k.par[b, label].astype(F32), parent)
+        grand = jnp.zeros((512, 1), F32)
+        for label in range(13):
+            grand = jnp.where(parent == first + label, k.par[b, label].astype(F32), grand)
+        seg_row, pos_row = stacked[0:1], stacked[1:2]
+        for i in range(4):
+            r = slice(i * 128, (i + 1) * 128)
+            same = (
+                (seg_row == seg_col[r]) | (seg_row == parent[r]) | (seg_row == grand[r])
+            ) & (pos_row <= pos_col[r])
+            k.bias[b * 512 + i * 128:b * 512 + (i + 1) * 128, :] = jnp.where(same, 0.0, MASKED).astype(BF)
+            angle = pos_col[r] * k.freq[0:1, :]
+            sign = jnp.where(lane % 64 < 32, -1.0, 1.0)
+            k.cs[b * 512 + i * 128:b * 512 + (i + 1) * 128, 0:128] = jnp.cos(angle)
+            k.cs[b * 512 + i * 128:b * 512 + (i + 1) * 128, 128:256] = jnp.sin(angle) * sign
+
+    def first_ring():
+        ring["kvq"].pump()
+        ring["o"].pump()
+
+    def second_ring():
+        ring["g"].pump()
+        ring["u"].pump()
+
+    first_ring()
+    first_ring()
+    for b in range(MB):
+        ex["x", b].forward()
+    for b in range(MB):
+        ex["dy", b].start()
+    first_ring()
+    ring["g"].start()
+    ring["u"].start()
+    first_ring()
+    first_ring()
+    first_ring()
+    first_ring()
+    for copy in token_copies:
+        copy.wait()
+    for b in range(MB):
+        ex["x", b].finish()
+
+    for i in range(10):
+        turned = k.wa[i * 128:(i + 1) * 128, 512:640].astype(F32).T
+        k.gains[:, i * 128:(i + 1) * 128] = turned[64:72]
+
+    def normed(r):
+        source = k.xall[r, :].astype(F32)
+        scale = lax.rsqrt(jnp.mean(source * source, axis=-1, keepdims=True) + EPSILON)
+        return source * scale
+
+    def project(b):
+        def norm(i):
+            k.n2all[rows(i, 64, 64), :] = (normed(pl.ds(pl.multiple_of(b * 512 + i * 64, 64), 64)) * k.gains[0:1, :]).astype(BF)
+
+        loop(8, norm)
+
+        def body(i):
+            r = pl.ds(pl.multiple_of(b * 512 + i * 256, 256), 256)
+            out = dot(k.n2all[rows(i, 256, 256), :], k.wa[:, 0:QKV], 1, 0)
+            cos, sin = k.cs[r, 0:128], k.cs[r, 128:256]
+            key = out[:, 0:128]
+            key = key * cos + swap_halves(key) * sin
+            value = out[:, 128:256]
+            k.qkv[r, 0:128] = key.astype(BF)
+            k.kvrot[r, 0:128] = pltpu.roll(key, 64, 1).astype(BF)
+            k.qkv[r, 128:256] = value.astype(BF)
+            k.kvrot[r, 128:256] = pltpu.roll(value, 64, 1).astype(BF)
+            for chunk in range(3):
+                u = out[:, 256 + chunk * 128:384 + chunk * 128]
+                u = (u * cos + swap_halves(u) * sin) * HD ** (-0.5)
+                if chunk == 2:
+                    u = jnp.where(lax.broadcasted_iota(jnp.int32, u.shape, 1) < 64, u, 0.0)
+                k.qkv[r, 256 + chunk * 128:384 + chunk * 128] = u.astype(BF)
+
+        loop(2, body)
+
+    def head_masks(h):
+        parity = h % 2
+        group = jnp.where(h < 4 - t, 0, 1)
+        in_half = (lane // 64 == parity).astype(F32)
+        straight = (group == parity).astype(F32)
+        return parity, group, in_half, straight
+
+    def pick(b, h, lanes):
+        parity, group, in_half, straight = head_masks(h)
+        r = slice(b * 512, (b + 1) * 512)
+        keep = (in_half * straight).astype(BF)
+        turn = (in_half * (1.0 - straight)).astype(BF)
+        return k.qkv[r, lanes] * keep + k.kvrot[r, lanes] * turn
+
+    def chunk_of(h, base):
+        return pl.ds(pl.multiple_of(base + (h // 2) * 128, 128), 128)
+
+    def attend(b):
+        base = b * 512
+
+        def head(h):
+            keys, values = pick(b, h, slice(0, 128)), pick(b, h, slice(128, 256))
+            q = k.qkv[base:base + 512, chunk_of(h, 256)]
+            for low, high, width in ((0, 128, 128), (128, 512, 512)):
+                s = dot(q[low:high], keys[0:width], 1, 1) + k.bias[base + low:base + high, 0:width].astype(F32)
+                e = jnp.exp(s - jnp.max(s, axis=-1, keepdims=True))
+                prob = (e / jnp.sum(e, axis=-1, keepdims=True)).astype(BF)
+                k.prob[b * 5 + h, low:high, 0:width] = prob
+                out = dot(prob, values[0:width], 1, 0)
+                old = k.att[base + low:base + high, chunk_of(h, 0)].astype(F32)
+                k.att[base + low:base + high, chunk_of(h, 0)] = (jnp.where(h % 2 == 1, old, 0.0) + out).astype(BF)
+
+        loop(5, head)
+
+    def put_part(b, i, value):
+        for c in range(2):
+            k.part[b, c, i] = value[c * 128:(c + 1) * 128].astype(BF)
+
+    def two_blocks(b, body):
+        def step(i):
+            r = pl.ds(pl.multiple_of(b * 512 + i * 256, 256), 256)
+            put_part(b, i, body(r))
+
+        loop(2, step)
+
+    sums = {}
+
+    def tree_sum(name, tag, keep, b):
+        sums[name, b] = TreeSum(k, tag + b, keep, b)
+        sums[name, b].start()
+
+    def out_proj(b):
+        two_blocks(b, lambda r: dot(k.att[r, :], k.wa[:, QKV:AW], 1, 1))
+        tree_sum("hid", 0, 0, b)
+
+    def finish_hidden(b):
+        sums["hid", b].wait()
+
+        def body(i):
+            r = rows(i, 32, 32)
+            own = pl.ds(pl.multiple_of(b * 512 + t * 128 + i * 32, 32), 32)
+            hid = k.xall[own, :].astype(F32) + sums["hid", b].value(r)
+            k.hid[pl.ds(pl.multiple_of(b * 128 + i * 32, 32), 32), :] = hid
+            scale = lax.rsqrt(jnp.mean(hid * hid, axis=-1, keepdims=True) + EPSILON)
+            k.n2all[own, :] = (hid * scale * k.gains[1:2, :]).astype(BF)
+
+        loop(4, body)
+        ex["n2", b].start()
+        sums["hid", b].drain()
+
+    project(0)
+    project(1)
+    second_ring()
+    attend(0)
+    out_proj(0)
+    ring["d"].start()
+    second_ring()
+    attend(1)
+    sums["hid", 0].middle()
+    out_proj(1)
+    second_ring()
+    finish_hidden(0)
+    sums["hid", 1].middle()
+    for b in range(MB):
+        ex["dy", b].forward()
+    second_ring()
+    ex["n2", 0].forward()
+    finish_hidden(1)
+    second_ring()
+    ex["n2", 1].forward()
+    for b in range(MB):
+        ex["dy", b].finish()
+    second_ring()
+    second_ring()
+    ex["n2", 0].finish()
+    if stop != "fwd":
+        backward(k, ex, ring, sums, tree_sum, two_blocks, normed, pick, head_masks, chunk_of, cross, kv_copies)
+    else:
+        ex["n2", 1].finish()
+        for _ in range(7):
+            ring["d"].pump()
+        for name in ("x", "dy", "n2"):
+            for b in range(MB):
+                ex[name, b].drain()
+        for copy in kv_copies:
+            copy.wait_send()
+    for piece in ring.values():
+        piece.drain()
+    for i, name in enumerate(debug):
+        copy = pltpu.make_async_copy(getattr(k, name), getattr(k, "dbg_" + name), k.loc.at[0])
+        copy.start()
+        copy.wait()
+
+
+def backward(k, ex, ring, sums, tree_sum, two_blocks, normed, pick, head_masks, chunk_of, cross, kv_copies):
+    f, t, n, shard = k.f, k.t, k.n, k.shard
+    lane = lax.broadcasted_iota(jnp.int32, (8, 128), 1)[0:1]
+    everything = slice(0, 1024)
+    scatter = {
+        "d0": RingSum(k, 0, k.gd, 0, 512, k.slot_d, k.out_d, 0),
+        "d1": RingSum(k, 1, k.gd, 512, 384, k.slot_d, k.out_d, 512),
+        "g0": RingSum(k, 2, k.ggu, 0, 512, k.slot_gu, k.out_g, 0),
+        "g1": RingSum(k, 3, k.ggu, 512, 384, k.slot_gu, k.out_g, 512),
+        "u0": RingSum(k, 4, k.ggu, 896, 512, k.slot_gu, k.out_u, 0),
+        "u1": RingSum(k, 5, k.ggu, 1408, 384, k.slot_gu, k.out_u, 512),
+        "o": RingSum(k, 6, k.wgu, 640, 384, k.slot_a, k.out_a, 640),
+        "a0": RingSum(k, 7, k.wgu, 0, 512, k.slot_a, k.out_a, 0),
+        "a1": RingSum(k, 8, k.wgu, 512, 128, k.slot_a, k.out_a, 512),
+    }
+
+    def start(*names):
+        for name in names:
+            scatter[name].start()
+
+    def pump(*names):
+        for name in names:
+            scatter[name].pump()
+
+    def gate_up(b):
+        def body(i):
+            r = pl.ds(pl.multiple_of(b * 512 + i * 128, 128), 128)
+            source = k.n2all[r, :]
+            gate = dot(source, k.wgu[:, 0:896], 1, 0)
+            up = dot(source, k.wgu[:, 896:1792], 1, 0)
+            s = 1.0 / (1.0 + jnp.exp(-gate))
+            silu = gate * s
+            k.m[r, :] = (silu * up).astype(BF)
+            k.ab[r, 0:896] = (up * s * (1.0 + gate * (1.0 - s))).astype(BF)
+            k.ab[r, 896:1792] = silu.astype(BF)
+
+        loop(4, body)
+
+    def grad_down():
+        def body(i):
+            k.gd[rows(i, 256, 256), :] = dot(k.dyall[:, rows(i, 256, 256)], k.m[...], 0, 0).astype(BF)
+
+        loop(5, body)
+
+    def hidden_grads(b):
+        def body(i):
+            r = pl.ds(pl.multiple_of(b * 512 + i * 128, 128), 128)
+            product = dot(k.dyall[r, :], k.wd[...], 1, 0)
+            k.ab[r, 0:896] = (product * k.ab[r, 0:896].astype(F32)).astype(BF)
+            k.ab[r, 896:1792] = (product * k.ab[r, 896:1792].astype(F32)).astype(BF)
+
+        loop(4, body)
+
+    def second_norm_part(b):
+        two_blocks(b, lambda r: dot(k.ab[r, :], k.wgu[...], 1, 1))
+        tree_sum("dn2", 2, 0, b)
+
+    def grad_gate_up():
+        def body(i):
+            left = k.n2all[:, rows(i, 256, 256)]
+            for low in (0, 896):
+                k.ggu[rows(i, 256, 256), low:low + 896] = dot(left, k.ab[:, low:low + 896], 0, 0).astype(BF)
+
+        loop(5, body)
+
+    def finish_hidden_grad(b):
+        total = sums["dn2", b]
+        total.wait()
+
+        def body(i):
+            r = rows(i, 32, 32)
+            own = pl.ds(pl.multiple_of(b * 512 + t * 128 + i * 32, 32), 32)
+            local = pl.ds(pl.multiple_of(b * 128 + i * 32, 32), 32)
+            grad, hid = total.value(r), k.hid[local, :]
+            scale = lax.rsqrt(jnp.mean(hid * hid, axis=-1, keepdims=True) + EPSILON)
+            k.ggain[1:2, :] += jnp.sum(hid * scale * grad, axis=0, keepdims=True)
+            weighted = k.gains[1:2, :] * grad
+            dh = (
+                k.dyall[own, :].astype(F32)
+                + scale * weighted
+                - hid * (scale * scale * scale) * jnp.mean(hid * weighted, axis=-1, keepdims=True)
+            )
+            k.out_x[local, :] = dh
+            k.dyall[own, :] = dh.astype(BF)
+
+        loop(4, body)
+        ex["dh", b].start()
+        total.drain()
+
+    def output_part(b):
+        two_blocks(b, lambda r: dot(k.m[r, :], k.wd[...], 1, 1))
+        tree_sum("out", 4, 1, b)
+
+    def finish_output(b):
+        total = sums["out", b]
+        total.wait()
+
+        def body(i):
+            r = rows(i, 32, 32)
+            local = pl.ds(pl.multiple_of(b * 128 + i * 32, 32), 32)
+            k.out_y[local, :] = (k.hid[local, :] + total.value(r)).astype(BF)
+
+        loop(4, body)
+        total.drain()
+
+    def grad_out():
+        def body(i):
+            k.wgu[rows(i, 256, 256), 640:1024] = dot(k.dyall[:, rows(i, 256, 256)], k.att[...], 0, 0).astype(BF)
+
+        loop(5, body)
+
+    def mixed_grad():
+        def body(i):
+            k.att[rows(i, 256, 256), :] = dot(k.dyall[rows(i, 256, 256), :], k.wa[:, 640:1024], 1, 0).astype(BF)
+
+        loop(4, body)
+
+    def attend_back(b):
+        base = b * 512
+        k.dq[...] = jnp.zeros_like(k.dq)
+        k.dkv[...] = jnp.zeros_like(k.dkv)
+
+        def head(h):
+            parity, group, in_half, straight = head_masks(h)
+            keys, values = pick(b, h, slice(0, 128)), pick(b, h, slice(128, 256))
+            for low, high, width in ((0, 128, 128), (128, 512, 512)):
+                q = k.qkv[base + low:base + high, chunk_of(h, 256)]
+                grad = k.att[base + low:base + high, chunk_of(h, 0)]
+                prob = k.prob[b * 5 + h, low:high, 0:width]
+                grad_prob = dot(grad, values[0:width], 1, 1)
+                wide = prob.astype(F32)
+                delta = jnp.sum(wide * grad_prob, axis=-1, keepdims=True)
+                ds = (wide * (grad_prob - delta)).astype(BF)
+                k.dq[low:high, chunk_of(h, 0)] += dot(ds, keys[0:width], 1, 0)
+                dk = dot(ds, q, 0, 0) * in_half
+                dv = dot(prob, grad, 0, 0) * in_half
+                k.dkv[0:width, 0:128] += jnp.where(group == parity, dk, pltpu.roll(dk, 64, 1))
+                k.dkv[0:width, 128:256] += jnp.where(group == parity, dv, pltpu.roll(dv, 64, 1))
+
+        loop(5, head)
+
+        def body(i):
+            r = pl.ds(pl.multiple_of(base + i * 128, 128), 128)
+            local = rows(i, 128, 128)
+            cos, sin = k.cs[r, 0:128], k.cs[r, 128:256]
+            u = k.dkv[local, 0:128]
+            k.qkv[r, 0:128] = (u * cos - swap_halves(u) * sin).astype(BF)
+            k.qkv[r, 128:256] = k.dkv[local, 128:256].astype(BF)
+            for chunk in range(3):
+                u = k.dq[local, chunk * 128:(chunk + 1) * 128]
+                u = (u * cos - swap_halves(u) * sin) * HD ** (-0.5)
+                k.qkv[r, 256 + chunk * 128:384 + chunk * 128] = u.astype(BF)
+
+        loop(4, body)
+
+    def first_norm_part(b):
+        two_blocks(b, lambda r: dot(k.qkv[r, :], k.wa[:, 0:QKV], 1, 1))
+        tree_sum("dn1", 6, 0, b)
+
+    def first_norm_again(b):
+        def body(i):
+            r = pl.ds(pl.multiple_of(b * 512 + i * 32, 32), 32)
+            unit = normed(r)
+            k.dyall[r, :] = (unit * k.gains[0:1, :]).astype(BF)
+            spot = pl.ds(pl.multiple_of((i % 4) * 32, 32), 32)
+            grad = k.part[b, (i // 4) % 2, i // 8, spot, :].astype(F32)
+            k.ggain[0:1, :] += jnp.sum(unit * grad, axis=0, keepdims=True)
+
+        loop(16, body)
+
+    def grad_first():
+        def body(i):
+            k.wgu[rows(i, 256, 256), 0:QKV] = dot(k.dyall[:, rows(i, 256, 256)], k.qkv[...], 0, 0).astype(BF)
+
+        loop(5, body)
+        for i in range(10):
+            r = slice(i * 128, (i + 1) * 128)
+            turned = jnp.concatenate(
+                [jnp.zeros((64, 128), F32), k.ggain[:, r], jnp.zeros((56, 128), F32)], axis=0).T
+            k.wgu[r, 512:640] = (k.wgu[r, 512:640].astype(F32) + turned).astype(BF)
+
+    def finish_input(b):
+        total = sums["dn1", b]
+        total.wait()
+
+        def body(i):
+            r = rows(i, 32, 32)
+            own = pl.ds(pl.multiple_of(b * 512 + t * 128 + i * 32, 32), 32)
+            local = pl.ds(pl.multiple_of(b * 128 + i * 32, 32), 32)
+            grad, source = total.value(r), k.xall[own, :].astype(F32)
+            scale = lax.rsqrt(jnp.mean(source * source, axis=-1, keepdims=True) + EPSILON)
+            weighted = k.gains[0:1, :] * grad
+            k.out_x[local, :] = (
+                k.out_x[local, :]
+                + scale * weighted
+                - source * (scale * scale * scale) * jnp.mean(source * weighted, axis=-1, keepdims=True)
+            )
+
+        loop(4, body)
+        total.drain()
+
+    D, GU, A = ("d0", "d1"), ("g0", "g1", "u0", "u1"), ("a0", "a1")
+    down = ring["d"]
+    k.ggain[...] = jnp.zeros_like(k.ggain)
+    gate_up(0)
+    down.pump()
+    ex["n2", 1].finish()
+    gate_up(1)
+    down.pump()
+    down.pump()
+    for b in range(MB):
+        ex["dy", b].drain()
+    grad_down()
+    start(*D)
+    for _ in range(4):
+        down.pump()
+    hidden_grads(0)
+    pump(*D)
+    second_norm_part(0)
+    hidden_grads(1)
+    pump(*D)
+    sums["dn2", 0].middle()
+    second_norm_part(1)
+    for name in ("g", "u"):
+        ring[name].drain()
+    grad_gate_up()
+    start(*GU)
+    sums["dn2", 1].middle()
+    pump(*D)
+    finish_hidden_grad(0)
+    pump(*D)
+    finish_hidden_grad(1)
+    pump(*D)
+    ex["dh", 0].forward()
+    pump(*GU)
+    output_part(0)
+    pump(*D)
+    ex["dh", 1].forward()
+    output_part(1)
+    sums["out", 0].middle()
+    pump(*D)
+    for b in range(MB):
+        ex["dh", b].finish()
+    grad_out()
+    start("o")
+    sums["out", 1].middle()
+    pump(*GU)
+    mixed_grad()
+    attend_back(0)
+    finish_output(0)
+    pump(*GU)
+    pump("o")
+    first_norm_part(0)
+    for b in range(MB):
+        ex["dh", b].drain()
+    first_norm_again(0)
+    finish_output(1)
+    pump(*GU)
+    sums["dn1", 0].middle()
+    attend_back(1)
+    pump(*GU)
+    pump("o")
+    first_norm_part(1)
+    first_norm_again(1)
+    grad_first()
+    start(*A)
+    sums["dn1", 1].middle()
+    pump("o")
+    pump(*GU)
+    finish_input(0)
+    pump(*A)
+    pump("o")
+    pump(*GU)
+    pump(*A)
+    pump("o")
+    finish_input(1)
+    pump(*A)
+    pump("o")
+    pump(*A)
+    pump("o")
+    pump(*A)
+    pump(*A)
+    pump(*A)
+
+    part_rows = shard // 4
+    for rank in range(4):
+        here = slice(rank * part_rows, (rank + 1) * part_rows)
+        k.kvsend[rank, :, 0:256] = k.out_a[here, 0:256]
+        k.kvsend[rank, :, 256:384] = k.out_a[here, 512:640]
+    tail = []
+    for i, peer in enumerate((k.sib, k.far, cross)):
+        tail.append(pltpu.make_async_remote_copy(
+            k.kvsend.at[peer], k.out_kv.at[t], k.kv_s.at[3 + i], k.kv_r.at[3 + i], (f, peer), MESH))
+    own = pltpu.make_async_copy(k.kvsend.at[t], k.out_kv.at[t], k.loc.at[9])
+    own.start()
+    for copy in tail:
+        copy.start()
+    for copy in tail:
+        copy.wait_recv()
+    own.wait()
+    for copy in tail + kv_copies:
+        copy.wait_send()
+    for name in ("x", "n2"):
+        for b in range(MB):
+            ex[name, b].drain()
+    for chunk in scatter.values():
+        chunk.drain()
+
+
+def layer(n, shard, arrays, debug=(), stop=None):
+    def shape(dims, kind=BF):
+        return jax.ShapeDtypeStruct(dims, kind)
+
+    inputs = ("xin", "dyin", "apre", "kv4", "gate", "up", "down", "seg", "pos", "par", "freq")
+    spaces = dict(xin=pl.ANY, dyin=pl.ANY, apre=pltpu.VMEM, kv4=pl.ANY, gate=pl.ANY, up=pl.ANY, down=pl.ANY,
+                  seg=pltpu.VMEM, pos=pltpu.VMEM, par=pltpu.SMEM, freq=pltpu.VMEM)
+    outputs = {
+        "out_y": shape((256, 1280)),
+        "out_x": shape((256, 1280), F32),
+        "out_d": shape((shard, 896), F32),
+        "out_g": shape((shard, 896), F32),
+        "out_u": shape((shard, 896), F32),
+        "out_a": shape((shard, AW), F32),
+        "out_kv": shape((4, shard // 4, 384), F32),
+    }
+    half = shard // 2
+    dma = pltpu.SemaphoreType.DMA
+    scratch = {
+        "wa": pltpu.VMEM((1280, AW), BF),
+        "wgu": pltpu.VMEM((1280, 1792), BF),
+        "wd": pltpu.VMEM((1280, 896), BF),
+        "xall": pltpu.VMEM((1024, 1280), BF),
+        "dyall": pltpu.VMEM((1024, 1280), BF),
+        "n2all": pltpu.VMEM((1024, 1280), BF),
+        "stage": pltpu.VMEM((shard, AW), BF),
+        "kvr": pltpu.VMEM((4, shard // 4, 384), BF),
+        "qkv": pltpu.VMEM((1024, QKV), BF),
+        "kvrot": pltpu.VMEM((1024, 256), BF),
+        "att": pltpu.VMEM((1024, 384), BF),
+        "prob": pltpu.VMEM((10, 512, 512), BF),
+        "bias": pltpu.VMEM((1024, 512), BF),
+        "cs": pltpu.VMEM((1024, 256), F32),
+        "gains": pltpu.VMEM((8, 1280), F32),
+        "ggain": pltpu.VMEM((8, 1280), F32),
+        "m": pltpu.VMEM((1024, 896), BF),
+        "ab": pltpu.VMEM((1024, 1792), BF),
+        "part": pltpu.VMEM((2, 2, 2, 128, 1280), BF),
+        "near": pltpu.VMEM((2, 2, 2, 128, 1280), BF),
+        "half": pltpu.VMEM((2, 2, 128, 1280), BF),
+        "far_in": pltpu.VMEM((2, 2, 128, 1280), BF),
+        "hid": pltpu.VMEM((256, 1280), F32),
+        "gd": pltpu.VMEM((1280, 896), BF),
+        "ggu": pltpu.VMEM((1280, 1792), BF),
+        "slot_d": pltpu.VMEM((2, n - 1, half, 896), BF),
+        "slot_gu": pltpu.VMEM((2, n - 1, half, 1792), BF),
+        "slot_a": pltpu.VMEM((2, n - 1, half, AW), BF),
+        "dq": pltpu.VMEM((512, 384), F32),
+        "dkv": pltpu.VMEM((512, 256), F32),
+        "kvsend": pltpu.VMEM((4, shard // 4, 384), F32),
+        "loc": dma((10,)),
+        "kv_s": dma((6,)), "kv_r": dma((6,)),
+        "ex_s": dma((8, 3)), "ex_r": dma((8, 3)),
+        "ts_s": dma((8, 2)), "ts_r": dma((8, 2)),
+        "ga_s": dma((10, n - 1)), "ga_r": dma((10, n - 1)),
+        "rs_s": dma((18, n - 1)), "rs_r": dma((18, n - 1)),
+    }
+    outs = dict(outputs)
+    for name in debug:
+        outs["dbg_" + name] = shape(scratch[name].shape, scratch[name].dtype)
+    names = inputs + tuple(outs) + tuple(scratch)
+    return pl.pallas_call(
+        functools.partial(layer_kernel, n, shard, names, debug, stop),
+        out_shape=tuple(outs.values()),
+        in_specs=[pl.BlockSpec(memory_space=spaces[name]) for name in inputs],
+        out_specs=tuple(
+            pl.BlockSpec(memory_space=pl.ANY if name.startswith("dbg_") else pltpu.VMEM) for name in outs),
+        scratch_shapes=list(scratch.values()),
+        compiler_params=pltpu.CompilerParams(
+            collective_id=0, has_side_effects=True, vmem_limit_bytes=67043328),
+        name="layer",
+    )(*arrays)
+
+
+def fused_device(mesh_n, debug, stop, inputs, cotangent, segment_ids, parents, positions, norm1_gain, w_query, w_key,
+                 w_value, w_out, norm2_gain, w_gate, w_up, w_down):
+    shard = w_query.shape[0]
+    apre = jnp.concatenate(
+        [jnp.zeros((shard, 256), BF), w_query, jnp.zeros((shard, 64), BF), w_out.T, jnp.zeros((shard, 64), BF)], axis=1)
+    quarter = shard // 4
+    gain_lanes = jnp.concatenate(
+        [jnp.zeros((quarter, 64), BF), norm1_gain[:, None], norm2_gain[:, None], jnp.zeros((quarter, 62), BF)], axis=1)
+    kv4 = jnp.stack([
+        jnp.concatenate([w_key[:, rank * 64:rank * 64 + 128], w_value[:, rank * 64:rank * 64 + 128], gain_lanes], axis=1)
+        for rank in range(4)])
+    steps = 1.0 / ROPE_BASE ** (jnp.arange(32, dtype=F32) / 32)
+    freq = jnp.broadcast_to(jnp.tile(steps, 4)[None], (8, 128))
+    outs = layer(mesh_n, shard, (
+        inputs, cotangent, apre, kv4, w_gate, w_up, w_down.T, segment_ids, positions, parents, freq), debug, stop)
+    y, gx, gd, gg, gu, ga, kv = outs[:7]
+    key = sum(jnp.pad(kv[rank, :, 0:128], ((0, 0), (rank * 64, 192 - rank * 64))) for rank in range(4))
+    value = sum(jnp.pad(kv[rank, :, 128:256], ((0, 0), (rank * 64, 192 - rank * 64))) for rank in range(4))
+    gains = jnp.sum(kv[:, :, 320:322], axis=0)
+    return (
+        y.reshape(2, 128, 1280), gx.reshape(2, 128, 1280), gains[:, 0], ga[:, 256:576], key, value,
+        ga[:, 640:960].T, gains[:, 1], gg, gu, gd.T) + tuple(outs[7:])
 
 
 def across_rows(left_side, right_side):
@@ -439,8 +1319,10 @@
         P("fsdp", "tp"),
         P("tp", "fsdp"),
     )
+    ring = mesh.shape["fsdp"]
+    body = functools.partial(fused_device, ring, (), None) if ring == 8 else per_device
     return jax.shard_map(
-        per_device,
+        body,
         mesh=mesh,
         in_specs=placed,
         out_specs=(

time: 1440 us -> 273 us (0.19)
  waiting for transfers between devices: 957 us -> 0 us
  Pallas kernels: 0 us -> 255 us
  blocking collectives: 234 us -> 0 us
  matrix products: 152 us -> 0 us
  other arithmetic: 41.1 us -> 3.15 us
  between operations: 21.6 us -> 0.72 us
    reduce_scatter x13 -> x0, waiting for transfers between devices: 561 us -> none  [the longest x6 111 us: rows_out(): lax.psum_scatter(term.astype(jnp.bfloat16), 'tp', scatter_dimension=0, ti...]
    pallas_call x0 -> x1, Pallas kernels: none -> 255 us  [layer(): pl.pallas_call(functools.partial(layer_kernel, n, shard, names, debug, st...]
    unnamed x36 -> x0, waiting for transfers between devices: 212 us -> none
    all_gather x11 -> x0, waiting for transfers between devices: 184 us -> none  [the longest x8 79.7 us: rows_in(): return lax.all_gather(values, 'tp', axis=0, tiled=True)]
    all_gather x4 -> x0, blocking collectives: 153 us -> none  [the longest x1 43.6 us: fetch_weights(): lax.all_gather(w_key, ('fsdp', 'tp'), axis=0, tiled=True)]
    dot_general x62 -> x0, matrix products: 152 us -> none  [the longest x14 42.9 us: across_rows(): lax.dot_general(left_side, right_side, (((0,), (0,)), ((), ())), preferre...]
    unnamed x2 -> x0, blocking collectives: 81.5 us -> none
    convert_element_type x9 -> x0, other arithmetic: 17 us -> none  [the longest x2 9.07 us: one_block(): (scale * probability * (grad_prob - row_delta)).astype(jnp.bfloat16)]
  transfers between devices with their start and end apart: 30 -> 0, of which waited for: 25 -> 0; matrix products, arithmetic and copies ran while one was open for 12% -> 0% of each run, Pallas kernels for 0% -> 0%
where the time goes in v1:
time: 273 us; the launch traced here: 272 us
  Pallas kernels  255 us (93%)
  local copies, waits for them, and re-layouts  13.5 us (5%)
  other arithmetic  3.15 us (1%)
    pallas_call x1, Pallas kernels, layer(): pl.pallas_call(functools.partial(layer_kernel, n, shard, names, debug, st...  255 us

profile of v1, /device:TPU:0, one launch (start us, length us, event | category | flops | bytes accessed | tf_op | source)
XLA Modules:
  0.0 272.5 jit_solution(9560864714635608384)
XLA Ops:
  0.7 0.1 broadcast_in_dim.27
  0.8 0.6 broadcast_in_dim.28.refs_10_
  1.3 0.8 copy.41
  2.1 0.8 copy.42
  2.9 0.9 fusion
  3.8 0.1 concatenate.21
  3.9 0.1 concatenate.22
  4.0 0.1 concatenate.24
  4.1 0.1 concatenate.23
  4.2 0.7 pad_maximum_fusion.refs_3_
  4.9 1.8 concatenate.20.refs_2_
  6.7 255.1 %layer.1 = (bf16[256,1280]{1,0:T(8,128)(2,1)}, f32[256,1280]{1,0:T(8,128)}, f32[160,896]{1,0:T(8,128)}, f32[160,896]{1,0:T(8,128)}, f32[160,896]{1,0:T(8,128)}, ...) custom-call(bf16[2,128,1280]{2,1,0:T(8,128)(2,1)} %refs_0_.1, bf16[2,128,1280]{2,1,0:T(8,128)(2,1)} %refs_1_.1, ...), custom_call_target="tpu_custom_call" | custom-call | tf_op jit(solution)/shard_map/layer/pallas_call | solution.py:860
  261.8 0.0 copy-start.1
  261.8 1.0 slice_reduce_fusion
  262.9 0.9 slice_bitcast_fusion.4
  263.7 0.7 slice_reduce_fusion.1
  264.4 0.0 copy-start
  264.4 0.7 pad_add_fusion
  265.2 0.7 pad_add_fusion.1
  265.9 1.9 slice_bitcast_fusion
  267.7 0.0 copy-done.1
  267.7 0.8 copy.54
  268.6 0.0 copy-done
  268.6 0.0 copy-start.4
  268.6 0.0 copy-start.3
  268.6 1.1 copy.55
  269.6 0.4 copy-done.4
  270.0 0.0 copy-start.2
  270.0 0.8 copy.56
  270.8 0.0 copy-done.3
  270.8 0.8 copy.57
  271.7 0.0 copy-done.2
  271.7 0.8 copy.58
  (6 shorter events, 0.0 us)
Async XLA Ops:
  261.8 5.9 %copy-start.1 = (bf16[256,1280]{1,0:T(8,128)(2,1)S(1)}, bf16[256,1280]{1,0:T(8,128)(2,1)}, u32[]{:S(2)}) copy-start(bf16[256,1280]{1,0:T(8,128)(2,1)} %get-tuple-element.18) | copy-start | bytes 1966084
  264.4 4.1 %copy-start = (f32[256,1280]{1,0:T(8,128)S(1)}, f32[256,1280]{1,0:T(8,128)}, u32[]{:S(2)}) copy-start(f32[256,1280]{1,0:T(8,128)} %get-tuple-element.19) | copy-start | bytes 3932164
  268.6 1.4 copy-start.4
  268.6 2.3 copy-start.3
  270.0 1.6 copy-start.2
